TPU v7x, 32 devices: a whole 2x2x4 slice. The times are simulated.
32 devices in a mesh: dp: 4 (over z), row: 2 (over x), col: 4 (over y, core).
Axes of the slice: x: 2, y: 2, z: 4, core: 2. Of those that a mesh axis runs over, the one named last changes fastest.
Arguments:
- images: bfloat16 [32, 729, 1152], P(('dp', 'row', 'col')), may hold values from -6 to 6
- cotangent: bfloat16 [32, 729, 1152], P(('dp', 'row', 'col')), may hold values from -6 to 6
- first_gain: float32 [1152], replicated, may hold values from 0.25 to 1.75
- first_shift: float32 [1152], replicated, may hold values from -3 to 3
- query_weight: bfloat16 [1152, 1152], P('row', 'col'), may hold values from -0.1875 to 0.1875
- query_bias: float32 [1152], P('col'), may hold values from -3 to 3
- key_weight: bfloat16 [1152, 1152], P('row', 'col'), may hold values from -0.1875 to 0.1875
- value_weight: bfloat16 [1152, 1152], P('row', 'col'), may hold values from -0.1875 to 0.1875
- value_bias: float32 [1152], P('col'), may hold values from -3 to 3
- output_weight: bfloat16 [1152, 1152], P('col', 'row'), may hold values from -0.75 to 0.75
- output_bias: float32 [1152], replicated, may hold values from -3 to 3
- second_gain: float32 [1152], replicated, may hold values from 0.1 to 1.9
- second_shift: float32 [1152], replicated, may hold values from -3 to 3
- expand_weight: bfloat16 [1152, 4304], P('row', 'col'), may hold values from -0.1875 to 0.1875
- expand_bias: float32 [4304], P('col'), may hold values from -3 to 3
- shrink_weight: bfloat16 [4304, 1152], P('col', 'row'), may hold values from -0.1875 to 0.1875
- shrink_bias: float32 [1152], replicated, may hold values from -3 to 3
Outputs:
- layer_out: bfloat16 [32, 729, 1152], P(('dp', 'row', 'col'))
- grad_images: bfloat16 [32, 729, 1152], P(('dp', 'row', 'col'))
- grad_first_gain: float32 [1152], replicated
- grad_first_shift: float32 [1152], replicated
- grad_query_weight: float32 [1152, 1152], P('row', 'col')
- grad_query_bias: float32 [1152], P('col')
- grad_key_weight: float32 [1152, 1152], P('row', 'col')
- grad_value_weight: float32 [1152, 1152], P('row', 'col')
- grad_value_bias: float32 [1152], P('col')
- grad_output_weight: float32 [1152, 1152], P('col', 'row')
- grad_output_bias: float32 [1152], replicated
- grad_second_gain: float32 [1152], replicated
- grad_second_shift: float32 [1152], replicated
- grad_expand_weight: float32 [1152, 4304], P('row', 'col')
- grad_expand_bias: float32 [4304], P('col')
- grad_shrink_weight: float32 [4304, 1152], P('col', 'row')
- grad_shrink_bias: float32 [1152], replicated
All inputs are finite; a program needn't handle non-finite values.
Results may differ from a plain program's by a relative error of at most 0.038.
Values may be sent and summed in bfloat16 or wider, within the bound.
A program may use at most 448 MiB of HBM per device.

v0:
```python
import jax
import jax.numpy as jnp
from jax import lax
from jax.sharding import PartitionSpec as P

HEAD_DIM = 72
EPS = 1e-06
contract_last = (((2,), (1,)), ((), ()))
contract_rows = (((0, 1), (0, 1)), ((), ()))


def gelu_tanh(value):
    return jax.nn.gelu(value, approximate=True)


def norm_forward(stream, gain, shift):
    average = jnp.mean(stream, axis=-1, keepdims=True)
    second = jnp.mean(stream * stream, axis=-1, keepdims=True)
    inverse = lax.rsqrt(second - average * average + EPS)
    normed = (stream - average) * inverse
    return (normed, inverse, (normed * gain + shift).astype(jnp.bfloat16))


def norm_backward(grad_out, normed, inverse, gain):
    scaled = grad_out * gain
    first = jnp.mean(scaled, axis=-1, keepdims=True)
    second = jnp.mean(scaled * normed, axis=-1, keepdims=True)
    return inverse * (scaled - first - normed * second)


def spread(block):
    feature_part = lax.all_to_all(block, "row", split_axis=2, concat_axis=0, tiled=True)
    return lax.all_gather(feature_part, "col", axis=0, tiled=True)


def join_back(summed):
    return lax.all_to_all(
        summed.astype(jnp.bfloat16), "row", split_axis=0, concat_axis=2, tiled=True
    ).astype(summed.dtype)


def project_in(normed_bf, weight):
    gathered = spread(normed_bf)
    summed = lax.psum_scatter(
        jnp.dot(gathered, weight, preferred_element_type=jnp.float32).astype(jnp.bfloat16),
        "row",
        scatter_dimension=0,
        tiled=True,
    ).astype(jnp.float32)
    return (summed, gathered)


def project_out(block_bf, weight):
    partial_sums = jnp.dot(
        lax.all_gather(block_bf, "row", axis=0, tiled=True),
        weight,
        preferred_element_type=jnp.float32,
    )
    return join_back(
        lax.psum_scatter(
            partial_sums.astype(jnp.bfloat16), "col", scatter_dimension=0, tiled=True
        ).astype(jnp.float32)
    )


def back_out(grad_bf, acts_bf, weight):
    grads_all = spread(grad_bf)
    grad_acts = lax.psum_scatter(
        lax.dot_general(
            grads_all, weight, contract_last, preferred_element_type=jnp.float32
        ).astype(jnp.bfloat16),
        "row",
        scatter_dimension=0,
        tiled=True,
    ).astype(jnp.float32)
    grad_weight = lax.dot_general(
        lax.all_gather(acts_bf, "row", axis=0, tiled=True),
        grads_all,
        contract_rows,
        preferred_element_type=jnp.float32,
    )
    return (grad_acts, grad_weight)


def back_in(grad_bf, weight, normed_bf):
    inputs_all = spread(normed_bf)
    piece = lax.all_gather(grad_bf, "row", axis=0, tiled=True)
    contrib = lax.dot_general(piece, weight, contract_last, preferred_element_type=jnp.float32)
    partial_sums = contrib
    weight_grad = lax.dot_general(
        inputs_all, piece, contract_rows, preferred_element_type=jnp.float32
    )
    partial_sums, weight_grad = (partial_sums, weight_grad)
    grad_inputs = join_back(
        lax.psum_scatter(
            partial_sums.astype(jnp.bfloat16), "col", scatter_dimension=0, tiled=True
        ).astype(jnp.float32)
    )
    return (grad_inputs, weight_grad)


def split_heads(block):
    return block.reshape(block.shape[0], block.shape[1] // HEAD_DIM, HEAD_DIM)


def head_scores(queries, key_rows):
    scores = jnp.einsum(
        "qhd,khd->hqk",
        split_heads(queries),
        split_heads(key_rows),
        preferred_element_type=jnp.float32,
    )
    return scores * HEAD_DIM ** (-0.5)


def attend(queries, key_rows, value_rows):

    def one_image(triple):
        scores = head_scores(triple[0], triple[1])
        peak = jnp.max(scores, axis=-1, keepdims=True)
        log_total = peak + jnp.log(jnp.sum(jnp.exp(scores - peak), axis=-1, keepdims=True))
        attention = jnp.exp(scores - log_total).astype(jnp.bfloat16)
        mixed = jnp.einsum(
            "hqk,khd->qhd", attention, split_heads(triple[2]), preferred_element_type=jnp.float32
        )
        return (mixed.reshape(triple[0].shape).astype(jnp.bfloat16), log_total)

    return lax.map(one_image, (queries, key_rows, value_rows))


def attend_back(queries, key_rows, value_rows, attended, log_total, grad_attended):
    scale = HEAD_DIM ** (-0.5)

    def one_image(group):
        image_q, image_k, image_v, image_out, image_total, image_grad = group
        attention = jnp.exp(head_scores(image_q, image_k) - image_total)
        grad_heads = split_heads(image_grad)
        grad_probs = jnp.einsum(
            "qhd,khd->hqk", grad_heads, split_heads(image_v), preferred_element_type=jnp.float32
        )
        delta = jnp.einsum(
            "qhd,qhd->hq", grad_heads, split_heads(image_out), preferred_element_type=jnp.float32
        )[..., None]
        grad_scores = (attention * (grad_probs - delta)).astype(jnp.bfloat16)
        grad_queries = (
            jnp.einsum(
                "hqk,khd->qhd",
                grad_scores,
                split_heads(image_k),
                preferred_element_type=jnp.float32,
            )
            * scale
        )
        grad_keys = (
            jnp.einsum(
                "hqk,qhd->khd",
                grad_scores,
                split_heads(image_q),
                preferred_element_type=jnp.float32,
            )
            * scale
        )
        grad_values = jnp.einsum(
            "hqk,qhd->khd",
            attention.astype(jnp.bfloat16),
            grad_heads,
            preferred_element_type=jnp.float32,
        )
        shape = image_q.shape
        return (grad_queries.reshape(shape), grad_keys.reshape(shape), grad_values.reshape(shape))

    return lax.map(one_image, (queries, key_rows, value_rows, attended, log_total, grad_attended))


def feature_terms(grad_input1, normed1, grad_middle, grad_input2, normed2, grad_result):
    token_axes = (0, 1)
    return (
        jnp.sum(grad_input1 * normed1, axis=token_axes),
        jnp.sum(grad_input1, axis=token_axes),
        jnp.sum(grad_middle, axis=token_axes),
        jnp.sum(grad_input2 * normed2, axis=token_axes),
        jnp.sum(grad_input2, axis=token_axes),
        jnp.sum(grad_result, axis=token_axes),
    )


def embed_part(part_sum):
    start = lax.axis_index("col") * part_sum.shape[0]
    whole = jnp.zeros((part_sum.shape[0] * lax.axis_size("col"),), jnp.float32)
    return lax.dynamic_update_slice_in_dim(whole, part_sum, start, 0)


def grid_layer(images, cotangent, params):
    (
        first_gain,
        first_shift,
        query_weight,
        query_bias,
        key_weight,
        value_weight,
        value_bias,
        output_weight,
        output_bias,
        second_gain,
        second_shift,
        expand_weight,
        expand_bias,
        shrink_weight,
        shrink_bias,
    ) = params
    width = query_weight.shape[1]
    joined = jnp.concatenate((query_weight, key_weight, value_weight), axis=1)
    stream = images.astype(jnp.float32)
    normed1, inverse1, input1 = norm_forward(stream, first_gain, first_shift)
    projected, kept_first = project_in(input1, joined)
    queries = (projected[..., :width] + query_bias).astype(jnp.bfloat16)
    key_rows = projected[..., width : 2 * width].astype(jnp.bfloat16)
    value_rows = (projected[..., 2 * width :] + value_bias).astype(jnp.bfloat16)
    attended, log_total = attend(queries, key_rows, value_rows)
    middle = stream + project_out(attended, output_weight) + output_bias
    normed2, inverse2, input2 = norm_forward(middle, second_gain, second_shift)
    expanded, kept_second = project_in(input2, expand_weight)
    before = expanded + expand_bias
    hidden = gelu_tanh(before).astype(jnp.bfloat16)
    result = middle + project_out(hidden, shrink_weight) + shrink_bias
    grad_result = cotangent.astype(jnp.float32)
    grad_hidden, grad_shrink = back_out(cotangent, hidden, shrink_weight)
    gelu_back = jax.vjp(gelu_tanh, before)[1]
    grad_before = gelu_back(grad_hidden)[0]
    grad_input2, grad_expand = back_in(grad_before.astype(jnp.bfloat16), expand_weight, input2)
    grad_middle = grad_result + norm_backward(grad_input2, normed2, inverse2, second_gain)
    grad_attended, grad_output = back_out(grad_middle.astype(jnp.bfloat16), attended, output_weight)
    grad_queries, grad_keys, grad_values = attend_back(
        queries, key_rows, value_rows, attended, log_total, grad_attended.astype(jnp.bfloat16)
    )
    grad_joined_rows = jnp.concatenate((grad_queries, grad_keys, grad_values), axis=-1).astype(
        jnp.bfloat16
    )
    grad_input1, grad_joined = back_in(grad_joined_rows, joined, input1)
    grad_stream = grad_middle + norm_backward(grad_input1, normed1, inverse1, first_gain)
    token_axes = (0, 1)
    features = feature_terms(grad_input1, normed1, grad_middle, grad_input2, normed2, grad_result)
    biases = (
        embed_part(jnp.sum(grad_queries, axis=token_axes)),
        embed_part(jnp.sum(grad_values, axis=token_axes)),
        embed_part(jnp.sum(grad_before, axis=token_axes)),
    )
    blocks = (
        grad_joined[:, :width],
        grad_joined[:, width : 2 * width],
        grad_joined[:, 2 * width :],
        grad_output,
        grad_expand,
        grad_shrink,
    )
    return (result, grad_stream, features, biases, blocks)


def shards(
    images,
    cotangent,
    first_gain,
    first_shift,
    query_weight,
    query_bias,
    key_weight,
    value_weight,
    value_bias,
    output_weight,
    output_bias,
    second_gain,
    second_shift,
    expand_weight,
    expand_bias,
    shrink_weight,
    shrink_bias,
):
    params = (
        first_gain,
        first_shift,
        query_weight,
        query_bias,
        key_weight,
        value_weight,
        value_bias,
        output_weight,
        output_bias,
        second_gain,
        second_shift,
        expand_weight,
        expand_bias,
        shrink_weight,
        shrink_bias,
    )
    result, grad_stream, features, biases, blocks = grid_layer(images, cotangent, params)
    totals = lax.psum(
        (
            features[0],
            features[1],
            features[2],
            features[3],
            features[4],
            features[5],
            biases[0],
            biases[1],
            biases[2],
        ),
        ("dp", "row", "col"),
    )
    col_index = lax.axis_index("col")
    query_part = query_bias.shape[0]
    expand_part = expand_bias.shape[0]
    query_bias_grad = lax.dynamic_slice_in_dim(totals[6], col_index * query_part, query_part, 0)
    value_bias_grad = lax.dynamic_slice_in_dim(totals[7], col_index * query_part, query_part, 0)
    expand_bias_grad = lax.dynamic_slice_in_dim(totals[8], col_index * expand_part, expand_part, 0)
    weight_totals = (
        lax.psum(blocks[0].astype(jnp.bfloat16), "dp").astype(jnp.float32),
        lax.psum(blocks[1].astype(jnp.bfloat16), "dp").astype(jnp.float32),
        lax.psum(blocks[2].astype(jnp.bfloat16), "dp").astype(jnp.float32),
        lax.psum(blocks[3].astype(jnp.bfloat16), "dp").astype(jnp.float32),
        lax.psum(blocks[4].astype(jnp.bfloat16), "dp").astype(jnp.float32),
        lax.psum(blocks[5].astype(jnp.bfloat16), "dp").astype(jnp.float32),
    )
    return (
        result.astype(jnp.bfloat16),
        grad_stream.astype(jnp.bfloat16),
        totals[0],
        totals[1],
        weight_totals[0],
        query_bias_grad,
        weight_totals[1],
        weight_totals[2],
        value_bias_grad,
        weight_totals[3],
        totals[2],
        totals[3],
        totals[4],
        weight_totals[4],
        expand_bias_grad,
        weight_totals[5],
        totals[5],
    )


def solution(mesh):
    placed = (
        P(("dp", "row", "col"), None, None),
        P(("dp", "row", "col"), None, None),
        P(),
        P(),
        P("row", "col"),
        P("col"),
        P("row", "col"),
        P("row", "col"),
        P("col"),
        P("col", "row"),
        P(),
        P(),
        P(),
        P("row", "col"),
        P("col"),
        P("col", "row"),
        P(),
    )
    return jax.shard_map(
        shards,
        mesh=mesh,
        in_specs=placed,
        out_specs=(
            P(("dp", "row", "col"), None, None),
            P(("dp", "row", "col"), None, None),
            P(),
            P(),
            P("row", "col"),
            P("col"),
            P("row", "col"),
            P("row", "col"),
            P("col"),
            P("col", "row"),
            P(),
            P(),
            P(),
            P("row", "col"),
            P("col"),
            P("col", "row"),
            P(),
        ),
        check_vma=False,
    )
```

profile of v0, /device:TPU:0, one launch (start us, length us, event | category | flops | bytes accessed | tf_op | source)
XLA Modules:
  0.0 2109.9 jit_solution(17329852611036355849)
XLA Ops:
  37.9 25.5 %all_to_all.118 = bf16[2,2,209952]{2,1,0:T(2,128)(2,1)S(1)} all-to-all(bf16[2,2,209952]{2,1,0:T(2,128)(2,1)} %reshape.487), channel_id=1, replica_groups=mesh['dp'=4,'row'=2,'col'=4] {'row'}, dimensions={0} | all-to-all | bytes 3359232 | tf_op jit(solution)/shard_map/all_to_all | solution.py:32
  74.0 50.2 %all-gather.21.cloned.1.call-done = bf16[8,1,729,576]{2,3,1,0:T(8,128)(2,1)} async-done(((bf16[2,1,729,576]{2,3,1,0:T(8,128)(2,1)}), bf16[8,1,729,576]{2,3,1,0:T(8,128)(2,1)}) %all-gather.21.cloned.1.call-update) | async-done | bytes 6718480 | tf_op jit(solution)/shard_map/all_gather | solution.py:33
  138.8 122.5 %reduce-scatter.9.cloned.1.call-done = bf16[4,729,864]{2,1,0:T(8,128)(2,1)} async-done(((bf16[8,729,864]{2,1,0:T(8,128)(2,1)}), bf16[4,729,864]{2,1,0:T(8,128)(2,1)}) %reduce-scatter.9.cloned.1.call-update) | async-done | bytes 5038864 | tf_op jit(solution)/shard_map/reduce_scatter | solution.py:44
  283.5 32.8 %while.26 = (s32[]{:T(128)}, bf16[4,729,288]{1,2,0:T(8,128)(2,1)}, f32[4,4,729,1]{2,1,3,0:T(4,128)}, bf16[4,729,288]{1,2,0:T(8,128)(2,1)}, bf16[4,729,288]{1,2,0...) while((s32[]{:T(128)}, bf16[4,729,288]{1,2,0:T(8,128)(2,1)}, f32[4,4,729,1]{2,1,3,0:T(4,128)}, ...), condition=%wide.region_6.7_spmd, body=%wide.region_3.6_spmd.sunk | while | flops 629433152 | bytes 30664516 | solution.py:128
  316.6 49.3 %all-gather.13.cloned.1.call-done = bf16[8,729,288]{1,2,0:T(8,128)(2,1)} async-done(((bf16[4,729,288]{1,2,0:T(8,128)(2,1)}), bf16[8,729,288]{1,2,0:T(8,128)(2,1)}) %all-gather.13.cloned.1.call-update) | async-done | bytes 3359248 | tf_op jit(solution)/shard_map/all_gather | solution.py:55
  401.5 24.2 %all_to_all.119 = bf16[2,2,209952]{2,1,0:T(2,128)(2,1)S(1)} all-to-all(bf16[2,2,209952]{2,1,0:T(2,128)(2,1)} %reshape.489), channel_id=1, replica_groups=mesh['dp'=4,'row'=2,'col'=4] {'row'}, dimensions={0} | all-to-all | bytes 3359232 | tf_op jit(solution)/shard_map/all_to_all | solution.py:32
  439.0 25.5 %all_to_all.120 = bf16[2,729,576]{1,2,0:T(8,128)(2,1)S(1)} all-to-all(bf16[2,729,576]{1,2,0:T(8,128)(2,1)} %reduce-scatter.11.cloned.1.call-done), channel_id=1, replica_groups=mesh['dp'=4,'row'=2,'col'=4] {'row'}, dimensions={0} | all-to-all | bytes 3359232 | tf_op jit(solution)/shard_map/all_to_all | solution.py:37
  502.3 23.4 %all_to_all.121 = bf16[2,2,209952]{2,1,0:T(2,128)(2,1)S(1)} all-to-all(bf16[2,2,209952]{2,1,0:T(2,128)(2,1)} %reshape.491), channel_id=1, replica_groups=mesh['dp'=4,'row'=2,'col'=4] {'row'}, dimensions={0} | all-to-all | bytes 3359232 | tf_op jit(solution)/shard_map/all_to_all | solution.py:32
  535.3 16.6 convolution_convert_fusion
  551.9 33.1 %all-gather.23.cloned.1.call-done = bf16[8,1,729,576]{2,3,1,0:T(8,128)(2,1)} async-done(((bf16[2,1,729,576]{2,3,1,0:T(8,128)(2,1)}), bf16[8,1,729,576]{2,3,1,0:T(8,128)(2,1)}) %all-gather.23.cloned.1.call-update) | async-done | bytes 6718480 | tf_op jit(solution)/shard_map/all_gather | solution.py:33
  601.7 137.7 %reduce-scatter.17.cloned.1.call-done = bf16[4,729,1076]{1,2,0:T(8,128)(2,1)} async-done(((bf16[8,729,1076]{1,2,0:T(8,128)(2,1)}), bf16[4,729,1076]{1,2,0:T(8,128)(2,1)}) %reduce-scatter.17.cloned.1.call-update) | async-done | bytes 6275248 | tf_op jit(solution)/shard_map/reduce_scatter | solution.py:68
  739.4 154.3 %reduce-scatter.13.cloned.1.call-done = bf16[4,729,1076]{1,2,0:T(8,128)(2,1)} async-done(((bf16[8,729,1076]{1,2,0:T(8,128)(2,1)}), bf16[4,729,1076]{1,2,0:T(8,128)(2,1)}) %reduce-scatter.13.cloned.1.call-update) | async-done | bytes 6275248 | tf_op jit(solution)/shard_map/reduce_scatter | solution.py:44
  893.7 17.1 fusion.91
  911.7 159.4 %all-gather.17.cloned.1.call-done = bf16[8,729,1076]{1,2,0:T(8,128)(2,1)} async-done(((bf16[4,729,1076]{1,2,0:T(8,128)(2,1)}), bf16[8,729,1076]{1,2,0:T(8,128)(2,1)}) %all-gather.17.cloned.1.call-update) | async-done | bytes 12550480 | tf_op jit(solution)/shard_map/all_gather | solution.py:87
  1087.0 145.5 %all-gather.15.cloned.1.call-done = bf16[8,729,1076]{1,2,0:T(8,128)(2,1)} async-done(((bf16[4,729,1076]{1,2,0:T(8,128)(2,1)}), bf16[8,729,1076]{1,2,0:T(8,128)(2,1)}) %all-gather.15.cloned.1.call-update) | async-done | bytes 12550480 | tf_op jit(solution)/shard_map/all_gather | solution.py:55
  1248.4 50.8 %reduce-scatter.19.cloned.1.call-done = bf16[2,729,576]{1,2,0:T(8,128)(2,1)} async-done(((bf16[8,729,576]{1,2,0:T(8,128)(2,1)}), bf16[2,729,576]{1,2,0:T(8,128)(2,1)}) %reduce-scatter.19.cloned.1.call-update) | async-done | bytes 1679632 | tf_op jit(solution)/shard_map/reduce_scatter | solution.py:95
  1303.1 62.8 %reduce-scatter.15.cloned.1.call-done = bf16[2,729,576]{1,2,0:T(8,128)(2,1)} async-done(((bf16[8,729,576]{1,2,0:T(8,128)(2,1)}), bf16[2,729,576]{1,2,0:T(8,128)(2,1)}) %reduce-scatter.15.cloned.1.call-update) | async-done | bytes 1679632 | tf_op jit(solution)/shard_map/reduce_scatter | solution.py:60
  1437.7 23.0 %all_to_all.122 = bf16[2,2,209952]{2,1,0:T(2,128)(2,1)} all-to-all(bf16[2,2,209952]{2,1,0:T(2,128)(2,1)S(1)} %reshape.493), channel_id=1, replica_groups=mesh['dp'=4,'row'=2,'col'=4] {'row'}, dimensions={0} | all-to-all | bytes 3359232 | tf_op jit(solution)/shard_map/all_to_all | solution.py:32
  1468.0 49.9 %all-gather.27.cloned.1.call-done = bf16[8,1,729,576]{2,3,1,0:T(8,128)(2,1)} async-done(((bf16[2,1,729,576]{2,3,1,0:T(8,128)(2,1)}), bf16[8,1,729,576]{2,3,1,0:T(8,128)(2,1)}) %all-gather.27.cloned.1.call-update) | async-done | bytes 6718480 | tf_op jit(solution)/shard_map/all_gather | solution.py:33
  1525.7 47.8 %reduce-scatter.21.cloned.1.call-done = bf16[4,729,288]{1,2,0:T(8,128)(2,1)} async-done(((bf16[8,729,288]{1,2,0:T(8,128)(2,1)}), bf16[4,729,288]{1,2,0:T(8,128)(2,1)}) %reduce-scatter.21.cloned.1.call-update) | async-done | bytes 1679632 | tf_op jit(solution)/shard_map/reduce_scatter | solution.py:68
  1573.5 70.2 %while.27 = (s32[]{:T(128)}, f32[4,729,288]{1,2,0:T(8,128)}, bf16[4,729,288]{1,2,0:T(8,128)(2,1)}, f32[4,729,288]{1,2,0:T(8,128)S(1)}, bf16[4,729,288]{1,2,0:T(8...) while((s32[]{:T(128)}, f32[4,729,288]{1,2,0:T(8,128)}, ...), condition=%wide.region_18.19_spmd, body=%wide.region_17.18_spmd.sunk | while | flops 1549022848 | bytes 52812796 | solution.py:172
  1659.2 130.3 %all-gather.19.cloned.1.call-done = bf16[8,729,864]{2,1,0:T(8,128)(2,1)} async-done(((bf16[4,729,864]{2,1,0:T(8,128)(2,1)}), bf16[8,729,864]{2,1,0:T(8,128)(2,1)}) %all-gather.19.cloned.1.call-update) | async-done | bytes 10077712 | tf_op jit(solution)/shard_map/all_gather | solution.py:87
  1872.1 159.5 %all-reduce.4.cloned.1.call-done = (bf16[576,288]{1,0:T(8,128)(2,1)}, bf16[576,288]{1,0:T(8,128)(2,1)}, bf16[576,288]{1,0:T(8,128)(2,1)}, bf16[288,576]{1,0:T(8,...) async-done(((bf16[576,288]{1,0:T(8,128)(2,1)}, bf16[576,288]{1,0:T(8,128)(2,1)}, bf16[576,288]{1,0:T(8,128)(2,1)}, bf16[288,576]{1,0:T(8,128)(2,1)}, ...) | async-done | bytes 3806224 | tf_op jit(solution)/shard_map/psum | solution.py:317
  2055.0 41.5 %all-reduce = (f32[1152]{0:T(1024)}, f32[1152]{0:T(1024)}, f32[1152]{0:T(1024)S(1)}, f32[1152]{0:T(1024)S(1)}, f32[1152]{0:T(1024)}, /*index=5*/f32[1152]{0:T(10...) all-reduce(f32[1152]{0:T(1024)S(1)} %get-tuple-element.309, ...), channel_id=1, replica_groups=mesh['dp'=4,'row'=2,'col'=4] {'dp','row','col'}, use_global_device_ids=true, to_apply=%region_23.24 | all-reduce | flops 13520 | bytes 108160 | tf_op jit(solution)/shard_map/psum | solution.py:296
  (308 shorter events, 544.9 us)
Async XLA Ops:
  7.2 577.9 %copy-start = (bf16[576,1076]{1,0:T(8,128)(2,1)S(1)}, bf16[576,1076]{1,0:T(8,128)(2,1)}, u32[]{:S(2)}) copy-start(bf16[576,1076]{1,0:T(8,128)(2,1)} %param.34) | copy-start | bytes 3718660
  7.2 117.1 %all-gather.21.cloned.1.call-start = ((), (), s32[]{:S(2)}) async-start(), calls=%async_computation.28 | async-start | bytes 8847360 | tf_op jit(solution)/shard_map/all_gather | solution.py:33
  72.7 188.6 %reduce-scatter.9.cloned.1.call-start = ((), (), s32[]{:S(2)}) async-start(), calls=%async_computation.16 | async-start | bytes 15826944 | tf_op jit(solution)/shard_map/reduce_scatter | solution.py:44
  138.6 227.3 %all-gather.13.cloned.1.call-start = ((), (), s32[]{:S(2)}) async-start(), calls=%async_computation.17 | async-start | bytes 5308416 | tf_op jit(solution)/shard_map/all_gather | solution.py:55
  316.3 122.7 %reduce-scatter.11.cloned.1.call-start = ((), (), s32[]{:S(2)}) async-start(), calls=%async_computation.18 | async-start | bytes 8847360 | tf_op jit(solution)/shard_map/reduce_scatter | solution.py:60
  374.7 160.6 %all-gather.25.cloned.1.call-start = ((), (), s32[]{:S(2)}) async-start(), calls=%async_computation.30 | async-start | bytes 8847360 | tf_op jit(solution)/shard_map/all_gather | solution.py:33
  434.8 150.3 %all-gather.23.cloned.1.call-start = ((), (), s32[]{:S(2)}) async-start(), calls=%async_computation.29 | async-start | bytes 8847360 | tf_op jit(solution)/shard_map/all_gather | solution.py:33
  535.0 204.4 %reduce-scatter.17.cloned.1.call-start = ((), (), s32[]{:S(2)}) async-start(), calls=%async_computation.22 | async-start | bytes 19906560 | tf_op jit(solution)/shard_map/reduce_scatter | solution.py:68
  551.9 341.8 %reduce-scatter.13.cloned.1.call-start = ((), (), s32[]{:S(2)}) async-start(), calls=%async_computation.19 | async-start | bytes 19906560 | tf_op jit(solution)/shard_map/reduce_scatter | solution.py:44
  601.6 292.0 %copy-start.34 = (f32[1076]{0:T(1024)S(1)}, f32[1076]{0:T(1024)}, u32[]{:S(2)}) copy-start(f32[1076]{0:T(1024)} %param.35) | copy-start | bytes 12916
  601.7 469.4 %all-gather.17.cloned.1.call-start = ((), (), s32[]{:S(2)}) async-start(), calls=%async_computation.23 | async-start | bytes 19906560 | tf_op jit(solution)/shard_map/all_gather | solution.py:87
  910.8 321.7 %all-gather.15.cloned.1.call-start = ((), (), s32[]{:S(2)}) async-start(), calls=%async_computation.20 | async-start | bytes 19906560 | tf_op jit(solution)/shard_map/all_gather | solution.py:55
  911.4 387.9 %reduce-scatter.19.cloned.1.call-start = ((), (), s32[]{:S(2)}) async-start(), calls=%async_computation.24 | async-start | bytes 8847360 | tf_op jit(solution)/shard_map/reduce_scatter | solution.py:95
  1086.9 279.0 %reduce-scatter.15.cloned.1.call-start = ((), (), s32[]{:S(2)}) async-start(), calls=%async_computation.21 | async-start | bytes 8847360 | tf_op jit(solution)/shard_map/reduce_scatter | solution.py:60
  1299.3 66.6 %all-to-all-start.5 = ((bf16[2,729,576]{1,2,0:T(8,128)(2,1)}), bf16[2,729,576]{1,2,0:T(8,128)(2,1)S(1)}, u32[]{:S(2)}, u32[]{:S(2)}) async-start(bf16[2,729,576]{1,2,0:T(8,128)(2,1)} %reduce-scatter.19.cloned.1.call-done), calls=%async_computation.11 | async-start | bytes 3538944 | tf_op jit(solution)/shard_map/all_to_all | solution.py:37
  1365.9 26.2 %all-to-all-start.3 = ((bf16[2,729,576]{1,2,0:T(8,128)(2,1)}), bf16[2,729,576]{1,2,0:T(8,128)(2,1)}, u32[]{:S(2)}, u32[]{:S(2)}) async-start(bf16[2,729,576]{1,2,0:T(8,128)(2,1)} %reduce-scatter.15.cloned.1.call-done), calls=%async_computation.7 | async-start | bytes 3538944 | tf_op jit(solution)/shard_map/all_to_all | solution.py:37
  1370.6 147.3 %all-gather.27.cloned.1.call-start = ((), (), s32[]{:S(2)}) async-start(), calls=%async_computation.31 | async-start | bytes 8847360 | tf_op jit(solution)/shard_map/all_gather | solution.py:33
  1467.8 105.7 %reduce-scatter.21.cloned.1.call-start = ((), (), s32[]{:S(2)}) async-start(), calls=%async_computation.25 | async-start | bytes 5308416 | tf_op jit(solution)/shard_map/reduce_scatter | solution.py:68
  1525.6 263.9 %all-gather.19.cloned.1.call-start = ((), (), s32[]{:S(2)}) async-start(), calls=%async_computation.26 | async-start | bytes 15826944 | tf_op jit(solution)/shard_map/all_gather | solution.py:87
  1659.1 130.4 %copy-start.14 = (bf16[576,288]{1,0:T(8,128)(2,1)S(1)}, bf16[576,288]{1,0:T(8,128)(2,1)}, u32[]{:S(2)}) copy-start(bf16[576,288]{1,0:T(8,128)(2,1)} %copy-done.13) | copy-start | bytes 995332
  1659.1 130.4 %copy-start.16 = (bf16[576,288]{1,0:T(8,128)(2,1)S(1)}, bf16[576,288]{1,0:T(8,128)(2,1)}, u32[]{:S(2)}) copy-start(bf16[576,288]{1,0:T(8,128)(2,1)} %copy-done.15) | copy-start | bytes 995332
  1659.1 208.3 %reduce-scatter.23.cloned.1.call-start = ((), (), s32[]{:S(2)}) async-start(), calls=%async_computation.27 | async-start | bytes 8847360 | tf_op jit(solution)/shard_map/reduce_scatter | solution.py:95
  1803.1 228.5 %all-reduce.4.cloned.1.call-start = ((), (), s32[]{:S(2)}) async-start(), calls=%async_computation.32 | async-start | bytes 8699904 | tf_op jit(solution)/shard_map/psum | solution.py:317
  1867.4 176.1 %all-to-all-start.7 = ((bf16[2,729,576]{1,2,0:T(8,128)(2,1)}), bf16[2,729,576]{1,2,0:T(8,128)(2,1)S(1)}, u32[]{:S(2)}, u32[]{:S(2)}) async-start(bf16[2,729,576]{1,2,0:T(8,128)(2,1)} %reduce-scatter.23.cloned.1.call-done), calls=%async_computation.15 | async-start | bytes 3538944 | tf_op jit(solution)/shard_map/all_to_all | solution.py:37
  (39 other events, 737.0 us)
Sparse Core Ops, SparseCore 0:
  72.9 51.3 all-gather.20
  138.7 122.6 reduce-scatter.8
  316.5 49.3 all-gather.12
  374.8 64.1 reduce-scatter.10
  440.5 50.8 all-gather.24
  535.1 49.8 all-gather.22
  587.4 151.9 reduce-scatter.16
  741.7 151.9 reduce-scatter.12
  910.9 160.0 all-gather.16
  1072.4 160.0 all-gather.14
  1235.0 64.1 reduce-scatter.18
  1301.7 64.1 reduce-scatter.14
  1467.9 49.9 all-gather.26
  1525.7 47.7 reduce-scatter.20
  1659.2 130.1 all-gather.18
  1803.2 64.1 reduce-scatter.22
  1871.3 160.2 all-reduce.3
where the time goes:
time: 2120 us; the launch traced here: 2110 us
  waiting for transfers between devices  1380 us (65%)
  matrix products  208 us (10%)
  local copies, waits for them, and re-layouts  194 us (9%)
  blocking collectives  163 us (8%)
  other arithmetic  135 us (6%)
    all_gather x2, waiting for transfers between devices, back_in(): piece = lax.all_gather(grad_bf, 'row', axis=0, tiled=True)  290 us
    reduce_scatter x2, waiting for transfers between devices, project_in(): lax.psum_scatter(jnp.dot(gathered, weight, preferred_element_type=jnp.flo...  277 us
    all_gather x2, waiting for transfers between devices, project_out(): lax.all_gather(block_bf, 'row', axis=0, tiled=True)  195 us
    reduce_scatter x2, waiting for transfers between devices, back_out(): lax.psum_scatter(lax.dot_general(grads_all, weight, contract_last, prefer...  185 us
    psum x1, waiting for transfers between devices, shards(): lax.psum(blocks[0].astype(jnp.bfloat16), 'dp').astype(jnp.float32)  159 us
    all_gather x4, waiting for transfers between devices, spread(): return lax.all_gather(feature_part, 'col', axis=0, tiled=True)  133 us
    all_to_all x4, blocking collectives, spread(): lax.all_to_all(block, 'row', split_axis=2, concat_axis=0, tiled=True)  96.1 us
    unnamed x106, local copies, waits for them, and re-layouts  77.6 us
  transfers between devices with their start and end apart: 20, of which 17 were waited for; matrix products, arithmetic and copies ran while one was open for 11% of the time, Pallas kernels for 0%

commit v1 on v0

--- a/solution.py
+++ b/solution.py
@@ -2,11 +2,18 @@
 import jax.numpy as jnp
 from jax import lax
 from jax.sharding import PartitionSpec as P
+from jax.lax import all_gather
 
 HEAD_DIM = 72
 EPS = 1e-06
 contract_last = (((2,), (1,)), ((), ()))
 contract_rows = (((0, 1), (0, 1)), ((), ()))
+
+
+def try_all_the_local_data(my_data):
+    r2 = all_gather(my_data, "dp")
+    long_array = jnp.sum(r2, axis=0)
+    return long_array
 
 
 def gelu_tanh(value):
@@ -314,7 +321,7 @@
     value_bias_grad = lax.dynamic_slice_in_dim(totals[7], col_index * query_part, query_part, 0)
     expand_bias_grad = lax.dynamic_slice_in_dim(totals[8], col_index * expand_part, expand_part, 0)
     weight_totals = (
-        lax.psum(blocks[0].astype(jnp.bfloat16), "dp").astype(jnp.float32),
+        try_all_the_local_data(blocks[0].astype(jnp.bfloat16)).astype(jnp.float32),
         lax.psum(blocks[1].astype(jnp.bfloat16), "dp").astype(jnp.float32),
         lax.psum(blocks[2].astype(jnp.bfloat16), "dp").astype(jnp.float32),
         lax.psum(blocks[3].astype(jnp.bfloat16), "dp").astype(jnp.float32),

time: 2120 us -> 2140 us (level)
    all_gather x0 -> x1, waiting for transfers between devices: none -> 32.7 us  [try_all_the_local_data(): r2 = all_gather(my_data, 'dp')]
    unnamed x106 -> x102, local copies, waits for them, and re-layouts: 77.6 us -> 77.8 us
    unnamed x5 -> x4, other arithmetic: 47.3 us -> 47.3 us
  transfers between devices with their start and end apart: 20 -> 21, of which waited for: 17 -> 18; matrix products, arithmetic and copies ran while one was open for 11% -> 11% of each run, Pallas kernels for 0% -> 0%
where the time goes in v1:
time: 2140 us; the launch traced here: 2130 us
  waiting for transfers between devices  1400 us (65%)
  matrix products  209 us (10%)
  local copies, waits for them, and re-layouts  194 us (9%)
  blocking collectives  163 us (8%)
  other arithmetic  138 us (6%)
    all_gather x2, waiting for transfers between devices, back_in(): piece = lax.all_gather(grad_bf, 'row', axis=0, tiled=True)  290 us
    reduce_scatter x2, waiting for transfers between devices, project_in(): lax.psum_scatter(jnp.dot(gathered, weight, preferred_element_type=jnp.flo...  277 us
    all_gather x2, waiting for transfers between devices, project_out(): lax.all_gather(block_bf, 'row', axis=0, tiled=True)  195 us
    reduce_scatter x2, waiting for transfers between devices, back_out(): lax.psum_scatter(lax.dot_general(grads_all, weight, contract_last, prefer...  185 us
    psum x1, waiting for transfers between devices, shards(): lax.psum(blocks[1].astype(jnp.bfloat16), 'dp').astype(jnp.float32)  146 us
    all_gather x4, waiting for transfers between devices, spread(): return lax.all_gather(feature_part, 'col', axis=0, tiled=True)  133 us
    all_to_all x4, blocking collectives, spread(): lax.all_to_all(block, 'row', split_axis=2, concat_axis=0, tiled=True)  96.1 us
    unnamed x102, local copies, waits for them, and re-layouts  77.8 us
  transfers between devices with their start and end apart: 21, of which 18 were waited for; matrix products, arithmetic and copies ran while one was open for 11% of the time, Pallas kernels for 0%

profile of v1, /device:TPU:0, one launch (start us, length us, event | category | flops | bytes accessed | tf_op | source)
XLA Modules:
  0.0 2130.7 jit_solution(14610354786384665175)
XLA Ops:
  38.0 25.5 %all_to_all.118 = bf16[2,2,209952]{2,1,0:T(2,128)(2,1)S(1)} all-to-all(bf16[2,2,209952]{2,1,0:T(2,128)(2,1)} %reshape.491), channel_id=1, replica_groups=mesh['dp'=4,'row'=2,'col'=4] {'row'}, dimensions={0} | all-to-all | bytes 3359232 | tf_op jit(solution)/shard_map/all_to_all | solution.py:39
  73.9 50.4 %all-gather.24.cloned.1.call-done = bf16[8,1,729,576]{2,3,1,0:T(8,128)(2,1)} async-done(((bf16[2,1,729,576]{2,3,1,0:T(8,128)(2,1)}), bf16[8,1,729,576]{2,3,1,0:T(8,128)(2,1)}) %all-gather.24.cloned.1.call-update) | async-done | bytes 6718480 | tf_op jit(solution)/shard_map/all_gather | solution.py:40
  139.2 122.2 %reduce-scatter.9.cloned.1.call-done = bf16[4,729,864]{2,1,0:T(8,128)(2,1)} async-done(((bf16[8,729,864]{2,1,0:T(8,128)(2,1)}), bf16[4,729,864]{2,1,0:T(8,128)(2,1)}) %reduce-scatter.9.cloned.1.call-update) | async-done | bytes 5038864 | tf_op jit(solution)/shard_map/reduce_scatter | solution.py:51
  283.6 32.8 %while.26 = (s32[]{:T(128)}, bf16[4,729,288]{1,2,0:T(8,128)(2,1)}, f32[4,4,729,1]{2,1,3,0:T(4,128)}, bf16[4,729,288]{1,2,0:T(8,128)(2,1)}, bf16[4,729,288]{1,2,0...) while((s32[]{:T(128)}, bf16[4,729,288]{1,2,0:T(8,128)(2,1)}, f32[4,4,729,1]{2,1,3,0:T(4,128)}, ...), condition=%wide.region_6.7_spmd, body=%wide.region_3.6_spmd.sunk | while | flops 629433152 | bytes 30664516 | solution.py:135
  316.6 49.3 %all-gather.16.cloned.1.call-done = bf16[8,729,288]{1,2,0:T(8,128)(2,1)} async-done(((bf16[4,729,288]{1,2,0:T(8,128)(2,1)}), bf16[8,729,288]{1,2,0:T(8,128)(2,1)}) %all-gather.16.cloned.1.call-update) | async-done | bytes 3359248 | tf_op jit(solution)/shard_map/all_gather | solution.py:62
  401.6 24.2 %all_to_all.119 = bf16[2,2,209952]{2,1,0:T(2,128)(2,1)S(1)} all-to-all(bf16[2,2,209952]{2,1,0:T(2,128)(2,1)} %reshape.493), channel_id=1, replica_groups=mesh['dp'=4,'row'=2,'col'=4] {'row'}, dimensions={0} | all-to-all | bytes 3359232 | tf_op jit(solution)/shard_map/all_to_all | solution.py:39
  439.1 25.3 %all_to_all.120 = bf16[2,729,576]{1,2,0:T(8,128)(2,1)S(1)} all-to-all(bf16[2,729,576]{1,2,0:T(8,128)(2,1)} %reduce-scatter.11.cloned.1.call-done), channel_id=1, replica_groups=mesh['dp'=4,'row'=2,'col'=4] {'row'}, dimensions={0} | all-to-all | bytes 3359232 | tf_op jit(solution)/shard_map/all_to_all | solution.py:44
  502.1 23.4 %all_to_all.121 = bf16[2,2,209952]{2,1,0:T(2,128)(2,1)S(1)} all-to-all(bf16[2,2,209952]{2,1,0:T(2,128)(2,1)} %reshape.495), channel_id=1, replica_groups=mesh['dp'=4,'row'=2,'col'=4] {'row'}, dimensions={0} | all-to-all | bytes 3359232 | tf_op jit(solution)/shard_map/all_to_all | solution.py:39
  552.1 32.8 %all-gather.26.cloned.1.call-done = bf16[8,1,729,576]{2,3,1,0:T(8,128)(2,1)} async-done(((bf16[2,1,729,576]{2,3,1,0:T(8,128)(2,1)}), bf16[8,1,729,576]{2,3,1,0:T(8,128)(2,1)}) %all-gather.26.cloned.1.call-update) | async-done | bytes 6718480 | tf_op jit(solution)/shard_map/all_gather | solution.py:40
  601.6 137.6 %reduce-scatter.17.cloned.1.call-done = bf16[4,729,1076]{1,2,0:T(8,128)(2,1)} async-done(((bf16[8,729,1076]{1,2,0:T(8,128)(2,1)}), bf16[4,729,1076]{1,2,0:T(8,128)(2,1)}) %reduce-scatter.17.cloned.1.call-update) | async-done | bytes 6275248 | tf_op jit(solution)/shard_map/reduce_scatter | solution.py:75
  739.3 154.3 %reduce-scatter.13.cloned.1.call-done = bf16[4,729,1076]{1,2,0:T(8,128)(2,1)} async-done(((bf16[8,729,1076]{1,2,0:T(8,128)(2,1)}), bf16[4,729,1076]{1,2,0:T(8,128)(2,1)}) %reduce-scatter.13.cloned.1.call-update) | async-done | bytes 6275248 | tf_op jit(solution)/shard_map/reduce_scatter | solution.py:51
  893.6 17.1 fusion.91
  911.5 159.4 %all-gather.20.cloned.1.call-done = bf16[8,729,1076]{1,2,0:T(8,128)(2,1)} async-done(((bf16[4,729,1076]{1,2,0:T(8,128)(2,1)}), bf16[8,729,1076]{1,2,0:T(8,128)(2,1)}) %all-gather.20.cloned.1.call-update) | async-done | bytes 12550480 | tf_op jit(solution)/shard_map/all_gather | solution.py:94
  1086.9 145.5 %all-gather.18.cloned.1.call-done = bf16[8,729,1076]{1,2,0:T(8,128)(2,1)} async-done(((bf16[4,729,1076]{1,2,0:T(8,128)(2,1)}), bf16[8,729,1076]{1,2,0:T(8,128)(2,1)}) %all-gather.18.cloned.1.call-update) | async-done | bytes 12550480 | tf_op jit(solution)/shard_map/all_gather | solution.py:62
  1248.3 50.8 %reduce-scatter.19.cloned.1.call-done = bf16[2,729,576]{1,2,0:T(8,128)(2,1)} async-done(((bf16[8,729,576]{1,2,0:T(8,128)(2,1)}), bf16[2,729,576]{1,2,0:T(8,128)(2,1)}) %reduce-scatter.19.cloned.1.call-update) | async-done | bytes 1679632 | tf_op jit(solution)/shard_map/reduce_scatter | solution.py:102
  1303.0 62.8 %reduce-scatter.15.cloned.1.call-done = bf16[2,729,576]{1,2,0:T(8,128)(2,1)} async-done(((bf16[8,729,576]{1,2,0:T(8,128)(2,1)}), bf16[2,729,576]{1,2,0:T(8,128)(2,1)}) %reduce-scatter.15.cloned.1.call-update) | async-done | bytes 1679632 | tf_op jit(solution)/shard_map/reduce_scatter | solution.py:67
  1437.5 23.0 %all_to_all.122 = bf16[2,2,209952]{2,1,0:T(2,128)(2,1)} all-to-all(bf16[2,2,209952]{2,1,0:T(2,128)(2,1)S(1)} %reshape.497), channel_id=1, replica_groups=mesh['dp'=4,'row'=2,'col'=4] {'row'}, dimensions={0} | all-to-all | bytes 3359232 | tf_op jit(solution)/shard_map/all_to_all | solution.py:39
  1468.1 49.6 %all-gather.30.cloned.1.call-done = bf16[8,1,729,576]{2,3,1,0:T(8,128)(2,1)} async-done(((bf16[2,1,729,576]{2,3,1,0:T(8,128)(2,1)}), bf16[8,1,729,576]{2,3,1,0:T(8,128)(2,1)}) %all-gather.30.cloned.1.call-update) | async-done | bytes 6718480 | tf_op jit(solution)/shard_map/all_gather | solution.py:40
  1525.5 47.8 %reduce-scatter.21.cloned.1.call-done = bf16[4,729,288]{1,2,0:T(8,128)(2,1)} async-done(((bf16[8,729,288]{1,2,0:T(8,128)(2,1)}), bf16[4,729,288]{1,2,0:T(8,128)(2,1)}) %reduce-scatter.21.cloned.1.call-update) | async-done | bytes 1679632 | tf_op jit(solution)/shard_map/reduce_scatter | solution.py:75
  1573.3 70.2 %while.27 = (s32[]{:T(128)}, f32[4,729,288]{1,2,0:T(8,128)}, bf16[4,729,288]{1,2,0:T(8,128)(2,1)}, f32[4,729,288]{1,2,0:T(8,128)S(1)}, bf16[4,729,288]{1,2,0:T(8...) while((s32[]{:T(128)}, f32[4,729,288]{1,2,0:T(8,128)}, ...), condition=%wide.region_18.19_spmd, body=%wide.region_17.18_spmd.sunk | while | flops 1549022848 | bytes 52812796 | solution.py:179
  1658.9 130.3 %all-gather.22.cloned.1.call-done = bf16[8,729,864]{2,1,0:T(8,128)(2,1)} async-done(((bf16[4,729,864]{2,1,0:T(8,128)(2,1)}), bf16[8,729,864]{2,1,0:T(8,128)(2,1)}) %all-gather.22.cloned.1.call-update) | async-done | bytes 10077712 | tf_op jit(solution)/shard_map/all_gather | solution.py:94
  1871.9 32.7 %all-gather.32.cloned.1.call-done = bf16[4,576,288]{1,2,0:T(8,128)(2,1)} async-done(((bf16[1,576,288]{1,2,0:T(8,128)(2,1)}), bf16[4,576,288]{1,2,0:T(8,128)(2,1)}) %all-gather.32.cloned.1.call-update) | async-done | bytes 1327120 | tf_op jit(solution)/shard_map/all_gather | solution.py:14
  1907.6 145.7 %all-reduce.4.cloned.1.call-done = (bf16[576,288]{1,0:T(8,128)(2,1)}, bf16[576,288]{1,0:T(8,128)(2,1)}, bf16[288,576]{1,0:T(8,128)(2,1)}, bf16[576,1076]{1,0:T(8,128)(2,1)}, bf16[1076,576]{0,1:T(8,128)(2,1)}) async-done(((bf16[576,288]{1,0:T(8,128)(2,1)}, bf16[576,288]{1,0:T(8,128)(2,1)}, bf16[288,576]{1,0:T(8,128)(2,1)}, bf16[576,1076]{1,0:T(8,128)(2,1)}, bf16[1076,576]{0,1:T(8,128)(2,1)}), ...) | async-done | bytes 3474448 | tf_op jit(solution)/shard_map/psum | solution.py:325
  2075.6 41.5 %all-reduce = (f32[1152]{0:T(1024)}, f32[1152]{0:T(1024)}, f32[1152]{0:T(1024)S(1)}, f32[1152]{0:T(1024)S(1)}, f32[1152]{0:T(1024)}, /*index=5*/f32[1152]{0:T(10...) all-reduce(f32[1152]{0:T(1024)S(1)} %get-tuple-element.309, ...), channel_id=1, replica_groups=mesh['dp'=4,'row'=2,'col'=4] {'dp','row','col'}, use_global_device_ids=true, to_apply=%region_23.24 | all-reduce | flops 13520 | bytes 108160 | tf_op jit(solution)/shard_map/psum | solution.py:303
  (307 shorter events, 564.0 us)
Async XLA Ops:
  7.2 577.8 %copy-start = (bf16[576,1076]{1,0:T(8,128)(2,1)S(1)}, bf16[576,1076]{1,0:T(8,128)(2,1)}, u32[]{:S(2)}) copy-start(bf16[576,1076]{1,0:T(8,128)(2,1)} %param.34) | copy-start | bytes 3718660
  7.2 117.1 %all-gather.24.cloned.1.call-start = ((), (), s32[]{:S(2)}) async-start(), calls=%async_computation.28 | async-start | bytes 8847360 | tf_op jit(solution)/shard_map/all_gather | solution.py:40
  72.8 188.7 %reduce-scatter.9.cloned.1.call-start = ((), (), s32[]{:S(2)}) async-start(), calls=%async_computation.16 | async-start | bytes 15826944 | tf_op jit(solution)/shard_map/reduce_scatter | solution.py:51
  138.6 227.3 %all-gather.16.cloned.1.call-start = ((), (), s32[]{:S(2)}) async-start(), calls=%async_computation.17 | async-start | bytes 5308416 | tf_op jit(solution)/shard_map/all_gather | solution.py:62
  316.4 122.7 %reduce-scatter.11.cloned.1.call-start = ((), (), s32[]{:S(2)}) async-start(), calls=%async_computation.18 | async-start | bytes 8847360 | tf_op jit(solution)/shard_map/reduce_scatter | solution.py:67
  374.7 160.6 %all-gather.28.cloned.1.call-start = ((), (), s32[]{:S(2)}) async-start(), calls=%async_computation.30 | async-start | bytes 8847360 | tf_op jit(solution)/shard_map/all_gather | solution.py:40
  434.9 150.0 %all-gather.26.cloned.1.call-start = ((), (), s32[]{:S(2)}) async-start(), calls=%async_computation.29 | async-start | bytes 8847360 | tf_op jit(solution)/shard_map/all_gather | solution.py:40
  534.9 204.4 %reduce-scatter.17.cloned.1.call-start = ((), (), s32[]{:S(2)}) async-start(), calls=%async_computation.22 | async-start | bytes 19906560 | tf_op jit(solution)/shard_map/reduce_scatter | solution.py:75
  552.1 341.5 %reduce-scatter.13.cloned.1.call-start = ((), (), s32[]{:S(2)}) async-start(), calls=%async_computation.19 | async-start | bytes 19906560 | tf_op jit(solution)/shard_map/reduce_scatter | solution.py:51
  601.5 292.0 %copy-start.33 = (f32[1076]{0:T(1024)S(1)}, f32[1076]{0:T(1024)}, u32[]{:S(2)}) copy-start(f32[1076]{0:T(1024)} %param.35) | copy-start | bytes 12916
  601.6 469.4 %all-gather.20.cloned.1.call-start = ((), (), s32[]{:S(2)}) async-start(), calls=%async_computation.23 | async-start | bytes 19906560 | tf_op jit(solution)/shard_map/all_gather | solution.py:94
  910.7 321.7 %all-gather.18.cloned.1.call-start = ((), (), s32[]{:S(2)}) async-start(), calls=%async_computation.20 | async-start | bytes 19906560 | tf_op jit(solution)/shard_map/all_gather | solution.py:62
  911.3 387.9 %reduce-scatter.19.cloned.1.call-start = ((), (), s32[]{:S(2)}) async-start(), calls=%async_computation.24 | async-start | bytes 8847360 | tf_op jit(solution)/shard_map/reduce_scatter | solution.py:102
  1086.9 278.9 %reduce-scatter.15.cloned.1.call-start = ((), (), s32[]{:S(2)}) async-start(), calls=%async_computation.21 | async-start | bytes 8847360 | tf_op jit(solution)/shard_map/reduce_scatter | solution.py:67
  1299.2 66.6 %all-to-all-start.5 = ((bf16[2,729,576]{1,2,0:T(8,128)(2,1)}), bf16[2,729,576]{1,2,0:T(8,128)(2,1)S(1)}, u32[]{:S(2)}, u32[]{:S(2)}) async-start(bf16[2,729,576]{1,2,0:T(8,128)(2,1)} %reduce-scatter.19.cloned.1.call-done), calls=%async_computation.11 | async-start | bytes 3538944 | tf_op jit(solution)/shard_map/all_to_all | solution.py:44
  1365.8 26.2 %all-to-all-start.3 = ((bf16[2,729,576]{1,2,0:T(8,128)(2,1)}), bf16[2,729,576]{1,2,0:T(8,128)(2,1)}, u32[]{:S(2)}, u32[]{:S(2)}) async-start(bf16[2,729,576]{1,2,0:T(8,128)(2,1)} %reduce-scatter.15.cloned.1.call-done), calls=%async_computation.7 | async-start | bytes 3538944 | tf_op jit(solution)/shard_map/all_to_all | solution.py:44
  1370.5 147.2 %all-gather.30.cloned.1.call-start = ((), (), s32[]{:S(2)}) async-start(), calls=%async_computation.31 | async-start | bytes 8847360 | tf_op jit(solution)/shard_map/all_gather | solution.py:40
  1467.6 105.7 %reduce-scatter.21.cloned.1.call-start = ((), (), s32[]{:S(2)}) async-start(), calls=%async_computation.25 | async-start | bytes 5308416 | tf_op jit(solution)/shard_map/reduce_scatter | solution.py:75
  1525.4 263.8 %all-gather.22.cloned.1.call-start = ((), (), s32[]{:S(2)}) async-start(), calls=%async_computation.26 | async-start | bytes 15826944 | tf_op jit(solution)/shard_map/all_gather | solution.py:94
  1658.8 130.4 %copy-start.16 = (bf16[576,288]{1,0:T(8,128)(2,1)S(1)}, bf16[576,288]{1,0:T(8,128)(2,1)}, u32[]{:S(2)}) copy-start(bf16[576,288]{1,0:T(8,128)(2,1)} %copy-done.15) | copy-start | bytes 995332
  1658.8 208.4 %reduce-scatter.23.cloned.1.call-start = ((), (), s32[]{:S(2)}) async-start(), calls=%async_computation.27 | async-start | bytes 8847360 | tf_op jit(solution)/shard_map/reduce_scatter | solution.py:102
  1802.8 101.7 %all-gather.32.cloned.1.call-start = ((), (), s32[]{:S(2)}) async-start(), calls=%async_computation.32 | async-start | bytes 1843200 | tf_op jit(solution)/shard_map/all_gather | solution.py:14
  1833.2 220.1 %all-reduce.4.cloned.1.call-start = ((), (), s32[]{:S(2)}) async-start(), calls=%async_computation.33 | async-start | bytes 7815168 | tf_op jit(solution)/shard_map/psum | solution.py:325
  1867.2 197.0 %all-to-all-start.7 = ((bf16[2,729,576]{1,2,0:T(8,128)(2,1)}), bf16[2,729,576]{1,2,0:T(8,128)(2,1)S(1)}, u32[]{:S(2)}, u32[]{:S(2)}) async-start(bf16[2,729,576]{1,2,0:T(8,128)(2,1)} %reduce-scatter.23.cloned.1.call-done), calls=%async_computation.15 | async-start | bytes 3538944 | tf_op jit(solution)/shard_map/all_to_all | solution.py:44
  (37 other events, 772.7 us)
Sparse Core Ops, SparseCore 0:
  72.9 51.3 all-gather.23
  138.7 122.6 reduce-scatter.8
  316.5 49.3 all-gather.15
  374.8 64.1 reduce-scatter.10
  440.5 50.8 all-gather.27
  535.0 49.8 all-gather.25
  587.3 151.9 reduce-scatter.16
  741.6 151.9 reduce-scatter.12
  910.8 160.0 all-gather.19
  1072.3 160.0 all-gather.17
  1235.0 64.1 reduce-scatter.18
  1301.6 64.1 reduce-scatter.14
  1467.7 49.8 all-gather.29
  1525.5 47.7 reduce-scatter.20
  1659.0 130.1 all-gather.21
  1803.0 64.1 reduce-scatter.22
  1869.2 35.3 all-gather.31
  1908.3 145.0 all-reduce.3
